TPU v7x, 32 devices: a whole 2x2x4 slice. The times are simulated.
32 devices in a mesh: grp: 4 (over z), fsdp: 4 (over y, x), tp: 2 (over core).
Axes of the slice: x: 2, y: 2, z: 4, core: 2. Of those that a mesh axis runs over, the one named last changes fastest.
Arguments:
- frames: bfloat16 [768, 5120], P('fsdp', 'grp'), may hold values from -6 to 6
- projector: bfloat16 [5120, 8192], P('grp', 'tp'), may hold values from -0.078125 to 0.078125
- text_token_embedding: bfloat16 [4096, 8192], P(('grp', 'fsdp'), 'tp'), may hold values from -6 to 6
- norm_gain_vector: float32 [8192], replicated, may hold values from 0.1 to 1.9
- frozen: bfloat16 [8192, 1024], P('fsdp', 'tp'), may hold values from -0.0625 to 0.0625
- adapter_down_map: bfloat16 [8192, 64], P('fsdp'), may hold values from -0.0625 to 0.0625
- adapter_up_map: bfloat16 [64, 1024], P(None, 'tp'), may hold values from -0.75 to 0.75
- clip_frame_length: int32 [4, 4, 4], P('fsdp'), may hold values from 1 to 24, as said below
- audio_first_token: int32 [4, 4, 4], P('fsdp'), may hold values from 0 to 255, as said below
- segment_document_index: int32 [4096], P(('grp', 'fsdp')), may hold values from 0 to 63, never falling along the last dimension, each value on 1 to 256 neighbouring positions
- keep_document_flags: int32 [64], replicated, may hold values 0 or 1
- cotangent: bfloat16 [4096, 1024], P(('grp', 'fsdp'), 'tp'), may hold values from -0.09375 to 0.09375
Outputs:
- value_output: bfloat16 [4096, 1024], P(('grp', 'fsdp'), 'tp')
- projector_grad: float32 [5120, 8192], P('grp', 'tp')
- down_map_gradient: float32 [8192, 64], P('tp')
- up_map_gradient: float32 [64, 1024], P(None, 'tp')
Inputs may be any that keep to these rules, and one draw needn't show every extreme that they name: `clip_frame_length`: entry [f, g, k] is the length of clip k of frame block f * 4 + g; the 4 clips of a block sum to 48, and one of them has exactly 24 frames. `audio_first_token`: entry [f, g, k] is the first token, among the 256 tokens of block k * 4 + f, of the audio slots of clip k of frame block f * 4 + g; the 4 clips that one token block takes lie in distinct aligned windows of 64 tokens.
All inputs are finite; a program needn't handle non-finite values.
Results may differ from a plain program's by a relative error of at most 0.018.
Values may be sent and summed in bfloat16 or wider, within the bound.
A program may use at most 128 MiB of HBM per device.

v0:
```python
import jax
import jax.numpy as jnp
from jax import lax
from jax.sharding import PartitionSpec as P

adapter_scale = 2.0
norm_eps = 1e-05
plane = ("fsdp", "tp")


def contract_leading(left_side, right_side):
    return lax.dot_general(
        left_side, right_side, (((0,), (0,)), ((), ())), preferred_element_type=jnp.float32
    )


def contract_trailing(left_side, right_side):
    return lax.dot_general(
        left_side, right_side, (((1,), (1,)), ((), ())), preferred_element_type=jnp.float32
    )


def block_perm(f_size, t_size, shift):
    pairs = []
    for f_src in range(f_size):
        for t_src in range(t_size):
            b = f_src * t_size + (t_src + shift) % t_size
            pairs.append((f_src * t_size + t_src, b % f_size * t_size + b // f_size))
    return pairs


def shards(
    frames,
    projector,
    text_token_embedding,
    norm_gain_vector,
    frozen,
    adapter_down_map,
    adapter_up_map,
    clip_frame_length,
    audio_first_token,
    segment_document_index,
    keep_document_flags,
    cotangent,
):
    g_idx, f_idx, t_idx = (lax.axis_index("grp"), lax.axis_index("fsdp"), lax.axis_index("tp"))
    f_size, t_size = (lax.axis_size("fsdp"), lax.axis_size("tp"))
    tok, width = text_token_embedding.shape
    groups = clip_frame_length.shape[1]
    block_frames = frames.shape[0]
    per_group = block_frames // groups
    cols = width // f_size
    full_width = width * t_size
    v_shard = frozen.shape[1]
    v_full = v_shard * t_size
    rank = adapter_down_map.shape[1]
    frames_all = lax.all_gather(frames, "fsdp", axis=0, tiled=True)
    clips = lax.all_gather(jnp.stack([clip_frame_length[0], audio_first_token[0]]), "fsdp", axis=0)
    text = lax.all_to_all(
        text_token_embedding.reshape(tok, f_size, cols).transpose(1, 0, 2),
        "fsdp",
        split_axis=0,
        concat_axis=0,
        tiled=True,
    )
    own_block = t_idx * f_size + f_idx
    own_j = lax.rem(own_block, t_size)
    frozen_own = jnp.zeros((cols, v_full), jnp.bfloat16)
    for shift in range(t_size):
        j = lax.rem(t_idx + shift, t_size)
        piece = lax.ppermute(
            lax.dynamic_slice_in_dim(frozen, j * cols, cols, 0),
            plane,
            block_perm(f_size, t_size, shift),
        )
        t_src = lax.rem(own_j - shift + t_size, t_size)
        frozen_own = lax.dynamic_update_slice_in_dim(frozen_own, piece, t_src * v_shard, 1)
    down_own = lax.ppermute(
        lax.dynamic_slice_in_dim(adapter_down_map, t_idx * cols, cols, 0),
        plane,
        block_perm(f_size, t_size, 0),
    )
    gain_own = lax.dynamic_slice_in_dim(norm_gain_vector, t_idx * width + f_idx * cols, cols, 0)
    sizes, firsts = (clips[:, 0], clips[:, 1])
    ends = jnp.cumsum(sizes, axis=2)
    pick = lax.broadcasted_iota(jnp.int32, sizes.shape, 2) == g_idx
    size_in = jnp.sum(jnp.where(pick, sizes, 0), axis=2)
    start_in = jnp.sum(jnp.where(pick, ends - sizes, 0), axis=2)
    first_in = jnp.sum(jnp.where(pick, firsts, 0), axis=2)
    base_row = lax.broadcasted_iota(jnp.int32, size_in.shape, 1) * per_group + start_in
    token_iota = lax.broadcasted_iota(jnp.int32, (f_size, tok, groups), 1)
    offset = token_iota - first_in[:, None, :]
    live = (offset >= 0) & (offset < size_in[:, None, :])
    is_audio = jnp.any(live, axis=2)
    row = jnp.sum(jnp.where(live, base_row[:, None, :] + offset, 0), axis=2)
    row = jnp.where(is_audio, row, -1)
    frame_iota = lax.broadcasted_iota(jnp.int32, (f_size, tok, block_frames), 2)
    take = (row[:, :, None] == frame_iota).astype(jnp.bfloat16)
    take_own = lax.dynamic_index_in_dim(take, f_idx, 0, keepdims=False)
    doc_iota = lax.broadcasted_iota(jnp.int32, (tok, keep_document_flags.shape[0]), 1)
    weight_tok = jnp.sum(
        jnp.where(segment_document_index[:, None] == doc_iota, keep_document_flags[None, :], 0),
        axis=1,
    )
    grad_out = cotangent * weight_tok.astype(jnp.bfloat16)[:, None]
    both = lax.all_gather(
        jnp.concatenate([grad_out, adapter_up_map], axis=0), "tp", axis=1, tiled=True
    )
    grad_full, up_full = (both[:tok], both[tok:])
    lora_tok = (adapter_scale * contract_trailing(grad_full, up_full)).astype(jnp.bfloat16)
    lora_plane = lax.all_gather(lora_tok, "fsdp", axis=0, tiled=True)
    grad_rows = lax.psum(contract_leading(take_own, grad_full).astype(jnp.bfloat16), "grp")
    grad_rows = lax.all_gather(grad_rows, "fsdp", axis=0, tiled=True)
    lora_rows = (adapter_scale * contract_trailing(grad_rows, up_full)).astype(jnp.bfloat16)
    grad_norm = contract_trailing(grad_rows, frozen_own) + contract_trailing(lora_rows, down_own)
    projector_own = lax.dynamic_slice_in_dim(projector, f_idx * cols, cols, 1)
    embedded = lax.psum(
        jnp.dot(frames_all, projector_own, preferred_element_type=jnp.float32).astype(jnp.bfloat16),
        "grp",
    )
    audio = lax.dot_general(
        take,
        embedded.reshape(f_size, block_frames, cols),
        (((2,), (1,)), ((0,), (0,))),
        preferred_element_type=jnp.float32,
    ).astype(jnp.bfloat16)
    x = jnp.where(is_audio[:, :, None], audio, text).reshape(f_size * tok, cols)
    x32 = x.astype(jnp.float32)
    e32 = embedded.astype(jnp.float32)
    stats = lax.psum(
        jnp.concatenate(
            [
                jnp.sum(x32 * x32, axis=1),
                jnp.sum(e32 * e32, axis=1),
                jnp.sum(e32 * gain_own[None, :] * grad_norm, axis=1),
            ]
        ),
        plane,
    )
    n_tok, n_frames = (f_size * tok, f_size * block_frames)
    inv_tok = lax.rsqrt(stats[:n_tok] / full_width + norm_eps)
    inv_frame = lax.rsqrt(stats[n_tok : n_tok + n_frames] / full_width + norm_eps)
    dots = inv_frame * stats[n_tok + n_frames :]
    frame_grad = (
        inv_frame[:, None] * gain_own[None, :] * grad_norm
        - e32 * (inv_frame * inv_frame * dots / full_width)[:, None]
    ).astype(jnp.bfloat16)
    frame_grad = lax.all_gather(frame_grad, "fsdp", axis=1, tiled=True)
    projector_grad = contract_leading(frames_all, frame_grad)
    normed = (x32 * inv_tok[:, None] * gain_own[None, :]).astype(jnp.bfloat16)
    low_part = jnp.dot(normed, down_own, preferred_element_type=jnp.float32)
    value_part = jnp.dot(normed, frozen_own, preferred_element_type=jnp.float32)
    value_part = value_part + adapter_scale * jnp.dot(
        low_part.astype(jnp.bfloat16), up_full, preferred_element_type=jnp.float32
    )
    value_part = value_part.astype(jnp.bfloat16).reshape(f_size, tok, t_size, v_shard)
    low_send = jnp.broadcast_to(
        low_part.astype(jnp.bfloat16).reshape(f_size, tok, 1, rank), (f_size, tok, t_size, rank)
    )
    sent = (
        jnp.concatenate([value_part, low_send], axis=3)
        .transpose(0, 2, 1, 3)
        .reshape(f_size * t_size, tok, v_shard + rank)
    )
    got = lax.all_to_all(sent, plane, split_axis=0, concat_axis=0, tiled=True)
    total = jnp.sum(got.astype(jnp.float32), axis=0)
    value_output = total[:, :v_shard].astype(jnp.bfloat16)
    low_half = total[:, v_shard:].astype(jnp.bfloat16)
    up_part = adapter_scale * contract_leading(low_half, grad_out)
    down_part = contract_leading(normed, lora_plane)
    down_sum, up_sum = lax.psum((down_part, up_part), "grp")
    gathered = lax.all_gather(
        jnp.concatenate([down_sum, up_sum.reshape(-1, rank)], axis=0), "fsdp", axis=0
    )
    down_map_gradient = gathered[:, :cols].reshape(width, rank)
    up_map_gradient = jnp.sum(gathered[:, cols:], axis=0).reshape(rank, v_shard)
    return (value_output, projector_grad, down_map_gradient, up_map_gradient)


def solution(mesh):
    in_specs = (
        P("fsdp", "grp"),
        P("grp", "tp"),
        P(("grp", "fsdp"), "tp"),
        P(),
        P("fsdp", "tp"),
        P("fsdp", None),
        P(None, "tp"),
        P("fsdp", None, None),
        P("fsdp", None, None),
        P(("grp", "fsdp")),
        P(),
        P(("grp", "fsdp"), "tp"),
    )
    out_specs = (P(("grp", "fsdp"), "tp"), P("grp", "tp"), P("tp", None), P(None, "tp"))
    return jax.shard_map(shards, mesh=mesh, in_specs=in_specs, out_specs=out_specs, check_vma=False)
```

profile of v0, /device:TPU:0, one launch (start us, length us, event | category | flops | bytes accessed | tf_op | source)
XLA Modules:
  0.0 499.5 jit_solution(9193602135876863072)
XLA Ops:
  9.5 9.7 %all-gather = s32[8,4,4]{2,1,0:T(4,128)S(1)} all-gather(s32[2,4,4]{2,1,0:T(4,128)S(1)} %pad_add_fusion), channel_id=2, replica_groups=mesh['grp'=4,'fsdp'=4,'tp'=2] {'fsdp'}, dimensions={0}, use_global_device_ids=true | all-gather | bytes 640 | tf_op jit(solution)/shard_map/all_gather | solution.py:58
  22.4 2.3 all_gather.30
  25.8 20.9 %all-gather.7.cloned.1.call-done = bf16[768,1280]{1,0:T(8,128)(2,1)} async-done(((bf16[192,1280]{1,0:T(8,128)(2,1)}), bf16[768,1280]{1,0:T(8,128)(2,1)}) %all-gather.7.cloned.1.call-update) | async-done | bytes 1966096 | tf_op jit(solution)/shard_map/all_gather | solution.py:57
  46.7 5.7 %fusion.12 = bf16[768,1024]{0,1:T(8,128)(2,1)} fusion(bf16[768,1280]{1,0:T(8,128)(2,1)} %all-gather.7.cloned.1.call-done, bf16[1280,4096]{1,0:T(8,128)(2,1)} %param.13, s32[]{:T(128)S(6)} %select_n.60), kind=kOutput, calls=%fused_computation.20 | convolution fusion | flops 2014052352 | bytes 6160388 | tf_op jit(solution)/shard_map/dot_general | solution.py:118
  52.5 82.0 %all-reduce.7.cloned.1.call-done = (bf16[768,1024]{0,1:T(8,128)(2,1)}, bf16[192,1024]{1,0:T(8,128)(2,1)}) async-done(((bf16[768,1024]{0,1:T(8,128)(2,1)}, bf16[192,1024]{1,0:T(8,128)(2,1)}), (bf16[768,1024]{0,1:T(8,128)(2,1)}, bf16[192,1024]{1,0:T(8,128)(2,1)})) %all-reduce.7.cloned.1.call-update) | async-done | bytes 1966096 | tf_op jit(solution)/shard_map/psum | solution.py:117
  134.5 3.3 copy.56
  137.8 2.4 copy.57
  140.2 3.6 all-to-all-start
  143.8 3.0 constant_dynamic-slice_fusion
  146.8 9.4 %collective-permute-start = (bf16[1024,512]{1,0:T(8,128)(2,1)}, bf16[1024,512]{1,0:T(8,128)(2,1)}, u32[]{:S(2)}, u32[]{:S(2)}) collective-permute-start(bf16[1024,512]{1,0:T(8,128)(2,1)} %get-tuple-element.30), channel_id=1, source_target_pairs={{0,0},{1,2},{2,4},{3,6},{4,1},{5,3},{6,5},{7,7},{8,8},{9,10},{10,1... | collective-permute-start | bytes 3145736 | tf_op jit(solution)/shard_map/ppermute | solution.py:71
  159.3 2.3 constant_dynamic-update-slice_fusion.1
  161.6 40.1 %collective-permute-done.1 = bf16[1024,512]{1,0:T(8,128)(2,1)} collective-permute-done((bf16[1024,512]{1,0:T(8,128)(2,1)}, bf16[1024,512]{1,0:T(8,128)(2,1)}, u32[]{:S(2)}, u32[]{:S(2)}) %collective-permute-start.1) | collective-permute-done | bytes 1048608 | tf_op jit(solution)/shard_map/ppermute | solution.py:71
  201.7 2.3 constant_dynamic-update-slice_fusion
  204.0 2.6 copy.55
  206.6 4.5 multiply_reduce_fusion
  211.2 4.3 fusion.16
  215.5 6.7 %fusion.2 = (f32[768]{0:T(1024)S(1)}, f32[768]{0:T(1024)S(1)}, f32[768,1024]{0,1:T(8,128)}) fusion(bf16[768,1024]{0,1:T(8,128)(2,1)S(1)} %copy-done.2, f32[1024]{0:T(1024)S(1)} %dynamic_slice.20, f32[768,1024]{0,1:T(8,128)} %fusion.16, bf16[768,1024]{1,0:T(8,128)(2,1)} %all-gather.9.cloned.1.call-done, bf16[1024,1024]{1,0:T(8,128)(2,1)} %constant_dynamic-update-slice_fusion), kind=kOutput, calls=%fused_computation.9 | convolution fusion | flops 1616116224 | bytes 11544576 | tf_op jit(solution)/shard_map/dot_general | solution.py:18
  222.2 27.2 %psum.37 = f32[2560]{0:T(1024)S(1)} all-reduce(f32[2560]{0:T(1024)S(1)} %pad_maximum_fusion.3), channel_id=1, replica_groups=mesh['grp'=4,'fsdp'=4,'tp'=2] {'fsdp','tp'}, use_global_device_ids=true, to_apply=%region_12.13 | all-reduce | flops 2560 | bytes 20480 | tf_op jit(solution)/shard_map/psum | solution.py:130
  249.3 2.6 fusion.1
  253.5 5.3 %add_convert_fusion = bf16[1024,1024]{1,0:T(8,128)(2,1)} fusion(f32[1024,1024]{1,0:T(8,128)S(1)} %fusion.23, bf16[1024,1024]{1,0:T(8,128)(2,1)S(1)} %fusion.1, bf16[1024,1024]{1,0:T(8,128)(2,1)} %constant_dynamic-update-slice_fusion), kind=kOutput, calls=%fused_computation.7 | convolution fusion | flops 2150629376 | bytes 10485760 | tf_op jit(solution)/shard_map/dot_general | solution.py:152
  258.7 4.5 reshape.66
  263.2 6.1 %copy.61 = bf16[4,256,2,512]{1,3,2,0:T(8,128)(2,1)} copy(bf16[4,256,2,512]{3,2,1,0:T(2,128)(2,1)} %reshape.66) | data formatting | bytes 4194304 | tf_op jit(solution)/shard_map/reshape | solution.py:156
  269.4 3.2 pad_maximum_fusion
  272.5 4.4 all-to-all-start.1
  277.2 32.5 %all_gather.33 = bf16[1024,64]{0,1:T(8,128)(2,1)S(1)} all-gather(bf16[256,64]{0,1:T(8,128)(2,1)S(1)} %fusion.17), channel_id=1, replica_groups=mesh['grp'=4,'fsdp'=4,'tp'=2] {'fsdp'}, dimensions={0}, use_global_device_ids=true | all-gather | bytes 163840 | tf_op jit(solution)/shard_map/all_gather | solution.py:111
  314.3 35.8 %all-reduce.5.cloned.1.call-done = (f32[512,64]{0,1:T(8,128)}, f32[1024,64]{0,1:T(8,128)}) async-done(((f32[512,64]{0,1:T(8,128)}, f32[1024,64]{0,1:T(8,128)}), (f32[512,64]{0,1:T(8,128)}, f32[1024,64]{0,1:T(8,128)})) %all-reduce.5.cloned.1.call-update) | async-done | bytes 393232 | tf_op jit(solution)/shard_map/psum | solution.py:171
  352.2 3.6 fusion.6
  356.7 26.3 %all-gather.13.cloned.1.call-done = f32[6144,64]{0,1:T(8,128)} async-done(((f32[1536,64]{0,1:T(8,128)}), f32[6144,64]{0,1:T(8,128)}) %all-gather.13.cloned.1.call-update) | async-done | bytes 1572880 | tf_op jit(solution)/shard_map/all_gather | solution.py:172
  383.0 2.4 reshape.73
  388.3 67.0 %all-gather.11.cloned.1.call-done = bf16[768,4096]{0,1:T(8,128)(2,1)} async-done(((bf16[768,1024]{0,1:T(8,128)(2,1)}), bf16[768,4096]{0,1:T(8,128)(2,1)}) %all-gather.11.cloned.1.call-update) | async-done | bytes 6291472 | tf_op jit(solution)/shard_map/all_gather | solution.py:148
  455.3 14.9 %convolution_bitcast_fusion = f32[1280,4096]{0,1:T(8,128)} fusion(bf16[768,4096]{0,1:T(8,128)(2,1)} %all-gather.11.cloned.1.call-done, bf16[768,1280]{1,0:T(8,128)(2,1)} %all-gather.7.cloned.1.call-done), kind=kOutput, calls=%fused_computation | convolution fusion | flops 8053063680 | bytes 29229056 | tf_op jit(solution)/shard_map/dot_general | solution.py:12
  470.2 22.4 %copy.65 = f32[1280,4096]{1,0:T(8,128)} copy(f32[1280,4096]{0,1:T(8,128)} %convolution_bitcast_fusion) | data formatting | bytes 41943040
  (70 shorter events, 21.9 us)
Async XLA Ops:
  7.2 149.1 %copy-start = (bf16[2048,64]{0,1:T(8,128)(2,1)S(1)}, bf16[2048,64]{0,1:T(8,128)(2,1)}, u32[]{:S(2)}) copy-start(bf16[2048,64]{0,1:T(8,128)(2,1)} %param.17) | copy-start | bytes 786436
  7.2 39.5 %all-gather.7.cloned.1.call-start = ((), (), s32[]{:S(2)}) async-start(), calls=%async_computation.2 | async-start | bytes 2457600 | tf_op jit(solution)/shard_map/all_gather | solution.py:57
  7.9 126.6 %all-reduce.7.cloned.1.call-start = ((), (), s32[]{:S(2)}) async-start(), calls=%async_computation.7 | async-start | bytes 3932160 | tf_op jit(solution)/shard_map/psum | solution.py:117
  52.5 158.7 %all-gather.9.cloned.1.call-start = ((), (), s32[]{:S(2)}) async-start(), calls=%async_computation.3 | async-start | bytes 1966080 | tf_op jit(solution)/shard_map/all_gather | solution.py:113
  140.2 66.4 %all-to-all-start = ((bf16[4,256,1024]{2,1,0:T(8,128)(2,1)}), bf16[4,256,1024]{2,1,0:T(8,128)(2,1)S(1)}, u32[]{:S(2)}, u32[]{:S(2)}) async-start(bf16[4,256,1024]{2,1,0:T(8,128)(2,1)} %bitcast.60), calls=%async_computation | async-start | bytes 4194304 | tf_op jit(solution)/shard_map/all_to_all | solution.py:59
  146.8 10.9 %collective-permute-start = (bf16[1024,512]{1,0:T(8,128)(2,1)}, bf16[1024,512]{1,0:T(8,128)(2,1)}, u32[]{:S(2)}, u32[]{:S(2)}) collective-permute-start(bf16[1024,512]{1,0:T(8,128)(2,1)} %get-tuple-element.30), channel_id=1, source_target_pairs={{0,0},{1,2},{2,4},{3,6},{4,1},{5,3},{6,5},{7,7},{8,8},{9,10},{10,1... | collective-permute-start | bytes 3145736 | tf_op jit(solution)/shard_map/ppermute | solution.py:71
  156.3 45.4 %collective-permute-start.1 = (bf16[1024,512]{1,0:T(8,128)(2,1)}, bf16[1024,512]{1,0:T(8,128)(2,1)}, u32[]{:S(2)}, u32[]{:S(2)}) collective-permute-start(bf16[1024,512]{1,0:T(8,128)(2,1)} %get-tuple-element.29), channel_id=1, source_target_pairs={{0,2},{1,0},{2,6},{3,4},{4,3},{5,1},{6,7},{7,5},{8,10},{9,8},{10,1... | collective-permute-start | bytes 3145736 | tf_op jit(solution)/shard_map/ppermute | solution.py:71
  156.3 54.8 %collective-permute-start.2 = (bf16[1024,64]{0,1:T(8,128)(2,1)S(1)}, bf16[1024,64]{0,1:T(8,128)(2,1)S(1)}, u32[]{:S(2)}, u32[]{:S(2)}) collective-permute-start(bf16[1024,64]{0,1:T(8,128)(2,1)S(1)} %constant_dynamic-slice_fusion.2), channel_id=1, source_target_pairs={{0,0},{1,2},{2,4},{3,6},{4,1},{5,3},{6,5},{7,7},{8,8},{9,10},{10,1... | collective-permute-start | bytes 393224 | tf_op jit(solution)/shard_map/ppermute | solution.py:78
  211.1 4.3 copy-start.2
  272.5 38.4 %all-to-all-start.1 = ((bf16[8,256,576]{1,2,0:T(8,128)(2,1)}), bf16[8,256,576]{1,2,0:T(8,128)(2,1)}, u32[]{:S(2)}, u32[]{:S(2)}) async-start(bf16[8,256,576]{1,2,0:T(8,128)(2,1)} %bitcast.59), calls=%async_computation.1 | async-start | bytes 4718592 | tf_op jit(solution)/shard_map/all_to_all | solution.py:165
  276.9 73.2 %all-reduce.5.cloned.1.call-start = ((), (), s32[]{:S(2)}) async-start(), calls=%async_computation.6 | async-start | bytes 786432 | tf_op jit(solution)/shard_map/psum | solution.py:171
  310.9 41.2 %copy-start.3 = (bf16[768,1024]{0,1:T(8,128)(2,1)S(1)}, bf16[768,1024]{0,1:T(8,128)(2,1)}, u32[]{:S(2)}) copy-start(bf16[768,1024]{0,1:T(8,128)(2,1)} %get-tuple-element.27) | copy-start | bytes 4718596
  314.3 68.8 %all-gather.13.cloned.1.call-start = ((), (), s32[]{:S(2)}) async-start(), calls=%async_computation.5 | async-start | bytes 1966080 | tf_op jit(solution)/shard_map/all_gather | solution.py:172
  351.9 103.4 %all-gather.11.cloned.1.call-start = ((), (), s32[]{:S(2)}) async-start(), calls=%async_computation.4 | async-start | bytes 7864320 | tf_op jit(solution)/shard_map/all_gather | solution.py:148
  470.2 22.4 %copy-start.1 = (bf16[2048,64]{0,1:T(8,128)(2,1)S(1)}, bf16[2048,64]{0,1:T(8,128)(2,1)}, u32[]{:S(2)}) copy-start(bf16[2048,64]{0,1:T(8,128)(2,1)} %param.17) | copy-start | bytes 786436
Sparse Core Ops, SparseCore 0:
  9.8 36.8 all-gather.6
  52.6 81.8 all-reduce.6
  136.3 52.9 all-gather.8
  314.4 35.6 all-reduce.4
  352.3 30.6 all-gather.12
  385.3 70.0 all-gather.10
where the time goes:
time: 502 us; the launch traced here: 499 us
  waiting for transfers between devices  273 us (54%)
  blocking collectives  71.6 us (14%)
  local copies, waits for them, and re-layouts  58.1 us (12%)
  matrix products  45.5 us (9%)
  starting transfers between devices  18.6 us (4%)
  other arithmetic  18.5 us (4%)
  between operations  14.3 us (3%)
    psum x1, waiting for transfers between devices, shards(): lax.psum(jnp.dot(frames_all, projector_own, preferred_element_type=jnp.fl...  82 us
    all_gather x1, waiting for transfers between devices, shards(): frame_grad = lax.all_gather(frame_grad, 'fsdp', axis=1, tiled=True)  67 us
    ppermute x2, waiting for transfers between devices, shards(): lax.ppermute(lax.dynamic_slice_in_dim(frozen, j * cols, cols, 0), plane,...  40.1 us
    psum x1, waiting for transfers between devices, shards(): down_sum, up_sum = lax.psum((down_part, up_part), 'grp')  35.8 us
    all_gather x1, blocking collectives, shards(): lora_plane = lax.all_gather(lora_tok, 'fsdp', axis=0, tiled=True)  32.5 us
    unnamed x13, local copies, waits for them, and re-layouts  28.2 us
    psum x1, blocking collectives, shards(): lax.psum(jnp.concatenate([jnp.sum(x32 * x32, axis=1), jnp.sum(e32 * e32,...  27.2 us
    all_gather x1, waiting for transfers between devices, shards(): lax.all_gather(jnp.concatenate([down_sum, up_sum.reshape(-1, rank)], axis...  26.3 us
  transfers between devices with their start and end apart: 11, of which 6 were waited for; matrix products, arithmetic and copies ran while one was open for 8% of the time, Pallas kernels for 0%

commit v1 on v0

--- a/solution.py
+++ b/solution.py
@@ -114,9 +114,14 @@
     lora_rows = (adapter_scale * contract_trailing(grad_rows, up_full)).astype(jnp.bfloat16)
     grad_norm = contract_trailing(grad_rows, frozen_own) + contract_trailing(lora_rows, down_own)
     projector_own = lax.dynamic_slice_in_dim(projector, f_idx * cols, cols, 1)
-    embedded = lax.psum(
-        jnp.dot(frames_all, projector_own, preferred_element_type=jnp.float32).astype(jnp.bfloat16),
-        "grp",
+    embedded = jnp.sum(
+        lax.all_gather(
+            jnp.dot(frames_all, projector_own, preferred_element_type=jnp.float32).astype(
+                jnp.bfloat16
+            ),
+            "grp",
+        ),
+        axis=0,
     )
     audio = lax.dot_general(
         take,

time: 502 us -> 562 us (1.12)
  waiting for transfers between devices: 273 us -> 312 us
  other arithmetic: 18.5 us -> 28.9 us
  local copies, waits for them, and re-layouts: 58.1 us -> 67.2 us
    all_gather x0 -> x1, waiting for transfers between devices: none -> 114 us  [shards(): lax.all_gather(jnp.dot(frames_all, projector_own, preferred_element_type=...]
    psum x1, waiting for transfers between devices: 82 us -> 36.7 us  [shards(): lax.psum(contract_leading(take_own, grad_full).astype(jnp.bfloat16), 'grp')]
    all_gather x1, waiting for transfers between devices: 20.9 us -> 0.02 us  [shards(): frames_all = lax.all_gather(frames, 'fsdp', axis=0, tiled=True)]
    all_gather x0 -> x1, local copies, waits for them, and re-layouts: none -> 12.3 us  [shards(): lax.all_gather(jnp.dot(frames_all, projector_own, preferred_element_type=...]
    reduce_sum x0 -> x1, other arithmetic: none -> 10.4 us  [shards(): jnp.sum(lax.all_gather(jnp.dot(frames_all, projector_own, preferred_eleme...]
    ppermute x2, waiting for transfers between devices: 40.1 us -> 34 us  [shards(): lax.ppermute(lax.dynamic_slice_in_dim(frozen, j * cols, cols, 0), plane,...]
    unnamed x13 -> x29, local copies, waits for them, and re-layouts: 28.2 us -> 29.2 us
  transfers between devices with their start and end apart: 11 -> 12, of which waited for: 6 -> 6; matrix products, arithmetic and copies ran while one was open for 8% -> 10% of each run, Pallas kernels for 0% -> 0%
where the time goes in v1:
time: 562 us; the launch traced here: 560 us
  waiting for transfers between devices  312 us (56%)
  blocking collectives  68.6 us (12%)
  local copies, waits for them, and re-layouts  67.2 us (12%)
  matrix products  45.4 us (8%)
  other arithmetic  28.9 us (5%)
  starting transfers between devices  21.6 us (4%)
  between operations  16.1 us (3%)
    all_gather x1, waiting for transfers between devices, shards(): lax.all_gather(jnp.dot(frames_all, projector_own, preferred_element_type=...  114 us
    all_gather x1, waiting for transfers between devices, shards(): frame_grad = lax.all_gather(frame_grad, 'fsdp', axis=1, tiled=True)  67.1 us
    psum x1, waiting for transfers between devices, shards(): lax.psum(contract_leading(take_own, grad_full).astype(jnp.bfloat16), 'grp')  36.7 us
    ppermute x2, waiting for transfers between devices, shards(): lax.ppermute(lax.dynamic_slice_in_dim(frozen, j * cols, cols, 0), plane,...  34 us
    psum x1, waiting for transfers between devices, shards(): down_sum, up_sum = lax.psum((down_part, up_part), 'grp')  33.4 us
    all_gather x1, blocking collectives, shards(): lora_plane = lax.all_gather(lora_tok, 'fsdp', axis=0, tiled=True)  32.5 us
    unnamed x29, local copies, waits for them, and re-layouts  29.2 us
    all_gather x1, waiting for transfers between devices, shards(): lax.all_gather(jnp.concatenate([down_sum, up_sum.reshape(-1, rank)], axis...  26 us
  transfers between devices with their start and end apart: 12, of which 6 were waited for; matrix products, arithmetic and copies ran while one was open for 10% of the time, Pallas kernels for 0%

profile of v1, /device:TPU:0, one launch (start us, length us, event | category | flops | bytes accessed | tf_op | source)
XLA Modules:
  0.0 559.8 jit_solution(13767436401614058581)
XLA Ops:
  9.6 9.7 %all-gather = s32[8,4,4]{2,1,0:T(4,128)S(1)} all-gather(s32[2,4,4]{2,1,0:T(4,128)S(1)} %pad_add_fusion), channel_id=2, replica_groups=mesh['grp'=4,'fsdp'=4,'tp'=2] {'fsdp'}, dimensions={0}, use_global_device_ids=true | all-gather | bytes 640 | tf_op jit(solution)/shard_map/all_gather | solution.py:58
  23.3 2.3 all_gather.38
  27.2 36.7 %all-reduce.4.cloned.1.call-done = bf16[192,1024]{1,0:T(8,128)(2,1)} async-done(((bf16[192,1024]{1,0:T(8,128)(2,1)}), bf16[192,1024]{1,0:T(8,128)(2,1)}) %all-reduce.4.cloned.1.call-update) | async-done | bytes 393232 | tf_op jit(solution)/shard_map/psum | solution.py:112
  64.0 5.9 %fusion.12 = bf16[768,1024]{0,1:T(8,128)(2,1)} fusion(bf16[768,1280]{1,0:T(8,128)(2,1)} %all-gather.9.cloned.1.call-done, bf16[1280,4096]{1,0:T(8,128)(2,1)} %param.13, s32[]{:T(128)S(6)} %select_n.60), kind=kOutput, calls=%fused_computation.20 | convolution fusion | flops 2014052352 | bytes 6160388 | tf_op jit(solution)/shard_map/dot_general | solution.py:119
  71.4 9.5 %collective-permute-start = (bf16[1024,512]{1,0:T(8,128)(2,1)}, bf16[1024,512]{1,0:T(8,128)(2,1)}, u32[]{:S(2)}, u32[]{:S(2)}) collective-permute-start(bf16[1024,512]{1,0:T(8,128)(2,1)} %get-tuple-element.32), channel_id=1, source_target_pairs={{0,0},{1,2},{2,4},{3,6},{4,1},{5,3},{6,5},{7,7},{8,8},{9,10},{10,1... | collective-permute-start | bytes 3145736 | tf_op jit(solution)/shard_map/ppermute | solution.py:71
  80.9 3.3 copy.62
  84.2 2.5 copy.63
  86.7 4.6 all-to-all-start
  96.4 2.3 constant_dynamic-update-slice_fusion.1
  98.8 34.0 %collective-permute-done.1 = bf16[1024,512]{1,0:T(8,128)(2,1)S(1)} collective-permute-done((bf16[1024,512]{1,0:T(8,128)(2,1)S(1)}, bf16[1024,512]{1,0:T(8,128)(2,1)S(1)}, u32[]{:S(2)}, u32[]{:S(2)}) %collective-permute-start.1) | collective-permute-done | bytes 1048608 | tf_op jit(solution)/shard_map/ppermute | solution.py:71
  133.9 4.5 fusion.16
  138.5 114.3 %all-gather.15.cloned.1.call-done = bf16[3072,1024]{0,1:T(8,128)(2,1)} async-done(((bf16[768,1024]{0,1:T(8,128)(2,1)}), bf16[3072,1024]{0,1:T(8,128)(2,1)}) %all-gather.15.cloned.1.call-update) | async-done | bytes 6291472 | tf_op jit(solution)/shard_map/all_gather | solution.py:118
  252.7 12.3 %reshape.73 = bf16[4,768,1024]{1,0,2:T(4,128)(2,1)} reshape(bf16[3072,1024]{0,1:T(8,128)(2,1)} %all-gather.15.cloned.1.call-done) | data formatting | bytes 12582912 | tf_op jit(solution)/shard_map/all_gather | solution.py:118
  265.1 10.4 %reduce_sum.108 = bf16[768,1024]{0,1:T(8,128)(2,1)S(1)} reduce(bf16[4,768,1024]{1,0,2:T(4,128)(2,1)} %reshape.73, bf16[]{:T(256)} %constant.63.clone.1), dimensions={0}, to_apply=%region_6.7 | reduce | flops 2359296 | bytes 7864322 | tf_op jit(solution)/shard_map/reduce_sum | solution.py:117
  276.5 5.3 multiply_reduce_fusion
  281.8 5.3 fusion.2
  287.1 24.1 %psum.29 = f32[2560]{0:T(1024)S(1)} all-reduce(f32[2560]{0:T(1024)S(1)} %pad_maximum_fusion.3), channel_id=1, replica_groups=mesh['grp'=4,'fsdp'=4,'tp'=2] {'fsdp','tp'}, use_global_device_ids=true, to_apply=%region_12.13 | all-reduce | flops 2560 | bytes 20480 | tf_op jit(solution)/shard_map/psum | solution.py:135
  311.3 2.6 fusion.1
  315.7 5.3 add_convert_fusion
  321.0 4.5 reshape.66
  325.5 6.2 %copy.66 = bf16[4,256,2,512]{1,3,2,0:T(8,128)(2,1)} copy(bf16[4,256,2,512]{3,2,1,0:T(2,128)(2,1)} %reshape.66) | data formatting | bytes 4194304 | tf_op jit(solution)/shard_map/reshape | solution.py:161
  331.7 3.2 pad_maximum_fusion
  334.8 4.4 all-to-all-start.1
  339.5 32.5 %all_gather.41 = bf16[1024,64]{0,1:T(8,128)(2,1)S(1)} all-gather(bf16[256,64]{0,1:T(8,128)(2,1)S(1)} %fusion.17), channel_id=1, replica_groups=mesh['grp'=4,'fsdp'=4,'tp'=2] {'fsdp'}, dimensions={0}, use_global_device_ids=true | all-gather | bytes 163840 | tf_op jit(solution)/shard_map/all_gather | solution.py:111
  373.2 2.2 reduce.2
  376.6 33.4 %all-reduce.6.cloned.1.call-done = (f32[512,64]{0,1:T(8,128)}, f32[1024,64]{0,1:T(8,128)}) async-done(((f32[512,64]{0,1:T(8,128)}, f32[1024,64]{0,1:T(8,128)}), (f32[512,64]{0,1:T(8,128)}, f32[1024,64]{0,1:T(8,128)})) %all-reduce.6.cloned.1.call-update) | async-done | bytes 393232 | tf_op jit(solution)/shard_map/psum | solution.py:176
  411.9 3.7 fusion.6
  416.4 26.0 %all-gather.17.cloned.1.call-done = f32[6144,64]{0,1:T(8,128)} async-done(((f32[1536,64]{0,1:T(8,128)}), f32[6144,64]{0,1:T(8,128)}) %all-gather.17.cloned.1.call-update) | async-done | bytes 1572880 | tf_op jit(solution)/shard_map/all_gather | solution.py:177
  442.4 2.4 reshape.74
  447.7 67.1 %all-gather.13.cloned.1.call-done = bf16[768,4096]{1,0:T(8,128)(2,1)} async-done(((bf16[768,1024]{1,0:T(8,128)(2,1)}), bf16[768,4096]{1,0:T(8,128)(2,1)}) %all-gather.13.cloned.1.call-update) | async-done | bytes 6291472 | tf_op jit(solution)/shard_map/all_gather | solution.py:153
  514.8 15.0 %convolution_bitcast_fusion = f32[1280,4096]{0,1:T(8,128)} fusion(bf16[768,4096]{1,0:T(8,128)(2,1)} %all-gather.13.cloned.1.call-done, bf16[768,1280]{1,0:T(8,128)(2,1)} %all-gather.9.cloned.1.call-done), kind=kOutput, calls=%fused_computation | convolution fusion | flops 8053063680 | bytes 29229056 | tf_op jit(solution)/shard_map/dot_general | solution.py:12
  529.7 22.4 %copy.70 = f32[1280,4096]{1,0:T(8,128)} copy(f32[1280,4096]{0,1:T(8,128)} %convolution_bitcast_fusion) | data formatting | bytes 41943040
  (91 shorter events, 26.0 us)
Async XLA Ops:
  8.0 85.3 %copy-start = (bf16[2048,64]{0,1:T(8,128)(2,1)S(1)}, bf16[2048,64]{0,1:T(8,128)(2,1)}, u32[]{:S(2)}) copy-start(bf16[2048,64]{0,1:T(8,128)(2,1)} %param.17) | copy-start | bytes 786436
  8.0 55.9 %all-reduce.4.cloned.1.call-start = ((), (), s32[]{:S(2)}) async-start(), calls=%async_computation.3 | async-start | bytes 786432 | tf_op jit(solution)/shard_map/psum | solution.py:112
  21.7 0.7 copy-start.7
  25.5 108.4 %copy-start.4 = (bf16[320,1024]{1,0:T(8,128)(2,1)}, bf16[320,1024]{1,0:T(8,128)(2,1)S(1)}, u32[]{:S(2)}) copy-start(bf16[320,1024]{1,0:T(8,128)(2,1)S(1)} %all_gather.38) | copy-start | bytes 1966084
  26.6 37.4 %all-gather.9.cloned.1.call-start = ((), (), s32[]{:S(2)}) async-start(), calls=%async_computation.2 | async-start | bytes 2457600 | tf_op jit(solution)/shard_map/all_gather | solution.py:57
  27.2 106.8 %all-gather.11.cloned.1.call-start = ((), (), s32[]{:S(2)}) async-start(), calls=%async_computation.4 | async-start | bytes 1966080 | tf_op jit(solution)/shard_map/all_gather | solution.py:113
  63.9 188.8 %all-gather.15.cloned.1.call-start = ((), (), s32[]{:S(2)}) async-start(), calls=%async_computation.6 | async-start | bytes 7864320 | tf_op jit(solution)/shard_map/all_gather | solution.py:118
  64.0 5.9 %copy-start.9 = (bf16[2048,512]{1,0:T(8,128)(2,1)S(1)}, bf16[2048,512]{1,0:T(8,128)(2,1)}, u32[]{:S(2)}) copy-start(bf16[2048,512]{1,0:T(8,128)(2,1)} %param.16) | copy-start | bytes 6291460
  71.4 23.4 %collective-permute-start = (bf16[1024,512]{1,0:T(8,128)(2,1)}, bf16[1024,512]{1,0:T(8,128)(2,1)}, u32[]{:S(2)}, u32[]{:S(2)}) collective-permute-start(bf16[1024,512]{1,0:T(8,128)(2,1)} %get-tuple-element.32), channel_id=1, source_target_pairs={{0,0},{1,2},{2,4},{3,6},{4,1},{5,3},{6,5},{7,7},{8,8},{9,10},{10,1... | collective-permute-start | bytes 3145736 | tf_op jit(solution)/shard_map/ppermute | solution.py:71
  86.7 4.6 copy-start.11
  86.7 189.8 %all-to-all-start = ((bf16[4,256,1024]{2,1,0:T(8,128)(2,1)}), bf16[4,256,1024]{2,1,0:T(8,128)(2,1)}, u32[]{:S(2)}, u32[]{:S(2)}) async-start(bf16[4,256,1024]{2,1,0:T(8,128)(2,1)} %bitcast.6), calls=%async_computation | async-start | bytes 4194304 | tf_op jit(solution)/shard_map/all_to_all | solution.py:59
  91.3 41.5 %collective-permute-start.1 = (bf16[1024,512]{1,0:T(8,128)(2,1)S(1)}, bf16[1024,512]{1,0:T(8,128)(2,1)S(1)}, u32[]{:S(2)}, u32[]{:S(2)}) collective-permute-start(bf16[1024,512]{1,0:T(8,128)(2,1)S(1)} %copy-done.11), channel_id=1, source_target_pairs={{0,2},{1,0},{2,6},{3,4},{4,3},{5,1},{6,7},{7,5},{8,10},{9,8},{10,1... | collective-permute-start | bytes 3145736 | tf_op jit(solution)/shard_map/ppermute | solution.py:71
  93.3 40.6 %collective-permute-start.2 = (bf16[1024,64]{0,1:T(8,128)(2,1)S(1)}, bf16[1024,64]{0,1:T(8,128)(2,1)S(1)}, u32[]{:S(2)}, u32[]{:S(2)}) collective-permute-start(bf16[1024,64]{0,1:T(8,128)(2,1)S(1)} %constant_dynamic-slice_fusion.2), channel_id=1, source_target_pairs={{0,0},{1,2},{2,4},{3,6},{4,1},{5,3},{6,5},{7,7},{8,8},{9,10},{10,1... | collective-permute-start | bytes 393224 | tf_op jit(solution)/shard_map/ppermute | solution.py:78
  276.5 5.3 copy-start.2
  276.5 5.3 copy-start.6
  276.5 5.3 copy-start.10
  313.9 1.1 copy-start.5
  334.8 38.4 %all-to-all-start.1 = ((bf16[8,256,576]{1,2,0:T(8,128)(2,1)}), bf16[8,256,576]{1,2,0:T(8,128)(2,1)}, u32[]{:S(2)}, u32[]{:S(2)}) async-start(bf16[8,256,576]{1,2,0:T(8,128)(2,1)} %bitcast.62), calls=%async_computation.1 | async-start | bytes 4718592 | tf_op jit(solution)/shard_map/all_to_all | solution.py:170
  339.2 70.8 %all-reduce.6.cloned.1.call-start = ((), (), s32[]{:S(2)}) async-start(), calls=%async_computation.8 | async-start | bytes 786432 | tf_op jit(solution)/shard_map/psum | solution.py:176
  372.0 3.4 copy-start.8
  373.2 38.6 %copy-start.3 = (bf16[768,1024]{1,0:T(8,128)(2,1)S(1)}, bf16[768,1024]{1,0:T(8,128)(2,1)}, u32[]{:S(2)}) copy-start(bf16[768,1024]{1,0:T(8,128)(2,1)} %copy-done.2) | copy-start | bytes 4718596
  376.6 65.8 %all-gather.17.cloned.1.call-start = ((), (), s32[]{:S(2)}) async-start(), calls=%async_computation.7 | async-start | bytes 1966080 | tf_op jit(solution)/shard_map/all_gather | solution.py:177
  411.8 103.0 %all-gather.13.cloned.1.call-start = ((), (), s32[]{:S(2)}) async-start(), calls=%async_computation.5 | async-start | bytes 7864320 | tf_op jit(solution)/shard_map/all_gather | solution.py:153
  529.7 22.4 %copy-start.1 = (bf16[2048,64]{0,1:T(8,128)(2,1)S(1)}, bf16[2048,64]{0,1:T(8,128)(2,1)}, u32[]{:S(2)}) copy-start(bf16[2048,64]{0,1:T(8,128)(2,1)} %param.17) | copy-start | bytes 786436
Sparse Core Ops, SparseCore 0:
  26.7 37.1 all-reduce.3
  376.7 33.2 all-reduce.5
Sparse Core Ops, SparseCore 1:
  28.9 34.2 all-gather.8
  64.9 56.6 all-gather.10
  123.6 129.1 all-gather.14
  411.9 30.5 all-gather.16
  444.8 69.9 all-gather.12
